TPU v7x, 32 devices: a whole 2x2x4 slice. The times are simulated.
32 devices in a mesh: tok: 8 (over z, x), mp: 4 (over y, core).
Axes of the slice: x: 2, y: 2, z: 4, core: 2. Of those that a mesh axis runs over, the one named last changes fastest.
Arguments:
- tokens: bfloat16 [3072, 2048], P('tok', 'mp'), may hold values from -120 to 120
- norm_gain: float32 [2048], replicated, may hold values from 0.5 to 1.5
- running_sq: float32 [2048], P('mp'), may hold values from 0.5 to 4
- gate_weight: bfloat16 [2048, 8192], P(None, 'mp'), may hold values from -0.125 to 0.125
- up_weight: bfloat16 [2048, 8192], P(None, 'mp'), may hold values from -0.125 to 0.125
- down_weight_t: bfloat16 [2048, 8192], P(None, 'mp'), may hold values from -0.0625 to 0.0625
- groups: int32 [192], P('tok'), may hold values from 0 to 23, as said below
- cotangent: bfloat16 [3072, 2048], P('tok', 'mp'), may hold values from -6 to 6
Outputs:
- block_out: bfloat16 [3072, 2048], P('tok', 'mp')
- grad_tokens: bfloat16 [3072, 2048], P('tok', 'mp')
- running_new: float32 [2048], P('mp')
- grad_gain: float32 [2048], P('mp')
- grad_gate: float32 [2048, 8192], P('tok', 'mp')
- grad_up: float32 [2048, 8192], P('tok', 'mp')
- grad_down_t: float32 [2048, 8192], P('tok', 'mp')
Inputs may be any that keep to these rules, and one draw needn't show every extreme that they name: Each of the 24 ghost groups holds exactly 8 blocks.
All inputs are finite; a program needn't handle non-finite values.
Results may differ from a plain program's by a relative error of at most 0.02.
Values may be sent and summed in bfloat16 or wider, within the bound.
A program may use at most 128 MiB of HBM per device.

v0:
```python
import functools

import jax
import jax.numpy as jnp
from jax import lax
from jax.experimental import pallas as pl
from jax.experimental.pallas import tpu as pltpu
from jax.sharding import PartitionSpec as P

GHOST = 128
BLK = 16
EPSILON = 1e-05
MOMENTUM = 0.1
Z = 4
CORES = 2
MESH = pl.DeviceIdType.MESH
F32 = jnp.float32
BF16 = jnp.bfloat16


def dot(a, b, ca=1, cb=0, precision=None):
    return lax.dot_general(
        a, b, (((ca,), (cb,)), ((), ())), precision=precision, preferred_element_type=F32
    )


def kernel(
    tok_count,
    mp_count,
    x_ref,
    gain_ref,
    run_ref,
    groups_ref,
    dy_ref,
    wg_hbm,
    wu_hbm,
    wd_hbm,
    bo_ref,
    gt_ref,
    rn_ref,
    gg_ref,
    dgate_hbm,
    dup_hbm,
    ddown_hbm,
    wa,
    wb,
    hg,
    dg,
    hidden,
    ggi,
    gl,
    ht,
    dt,
    rbuf,
    mp_recv,
    stage,
    sblk,
    stat_x,
    stat_z,
    part_x,
    part_z,
    own_b,
    own_g,
    w_sem,
    zs,
    zr,
    ys,
    yr,
    cs,
    cr,
    sx_s,
    sx_r,
    sz_s,
    sz_r,
    px_s,
    px_r,
    pz_s,
    pz_r,
    rs_s,
    rs_r,
    ms_s,
    ms_r,
    o_sem,
):
    rows_t, feat = x_ref.shape
    width = wa.shape[1]
    full = feat * mp_count
    xs = tok_count // Z
    rows = full // tok_count
    ys_count = mp_count // CORES
    nb = rows_t // BLK
    groups_total = rows_t * tok_count // GHOST

    me = lax.axis_index("tok")
    m = lax.axis_index("mp")
    z, x = me // xs, me % xs
    y, c = m // CORES, m % CORES

    def z_peer(k):
        zz = z + 0
        if k & 1:
            zz = zz + 1 - 2 * (zz % 2)
        if k & 2:
            zz = (zz + 2) % Z
        return (zz * xs + x, m)

    def x_peer(j):
        return (z * xs + (x + j) % xs, m)

    def y_peer(j):
        return (me, ((y + j) % ys_count) * CORES + c)

    core_peer = (me, y * CORES + (1 - c))

    def mp_peer(j):
        return (me, (m + j) % mp_count)

    def remote(src, dst, s, r, dev):
        return pltpu.make_async_remote_copy(
            src_ref=src, dst_ref=dst, send_sem=s, recv_sem=r, device_id=dev, device_id_type=MESH
        )

    load_a = pltpu.make_async_copy(wg_hbm, wa, w_sem.at[0])
    load_b = pltpu.make_async_copy(wu_hbm, wb, w_sem.at[1])
    load_a.start()
    load_b.start()

    barrier = pltpu.get_barrier_semaphore()
    greet = [z_peer(k) for k in range(1, Z)] + [x_peer(j) for j in range(1, xs)]
    greet += [mp_peer(j) for j in range(1, mp_count)]
    for dev in greet:
        pl.semaphore_signal(barrier, inc=1, device_id=dev, device_id_type=MESH)
    pl.semaphore_wait(barrier, len(greet))

    bufs = (hg, dg)

    def block(a, k, owner):
        col = pl.multiple_of(owner * feat, feat)
        return bufs[a].at[pl.ds(k * rows_t, rows_t), pl.ds(col, feat)]

    def z_copy(a, k):
        return remote(block(a, 0, m), block(a, k, m), zs.at[a, k], zr.at[a, k], z_peer(k))

    def y_copy(a, k, j):
        return remote(block(a, k, m), block(a, k, m), ys.at[a, k, j], yr.at[a, k, j], y_peer(j))

    def y_from(j):
        return ((y + ys_count - j) % ys_count) * CORES + c

    def y_wait(a, k, j):
        b = block(a, k, y_from(j))
        remote(b, b, ys.at[a, k, j], yr.at[a, k, j], y_peer(j)).wait_recv()

    def c_copy(a, k, i):
        b = block(a, k, y_from(i))
        return remote(b, b, cs.at[a, k, i], cr.at[a, k, i], core_peer)

    def c_wait(a, k, i):
        b = block(a, k, ((y + ys_count - i) % ys_count) * CORES + (1 - c))
        remote(b, b, cs.at[a, k, i], cr.at[a, k, i], core_peer).wait_recv()

    def forward_y(a, k):
        if k > 0:
            b = block(a, k, m)
            remote(b, b, zs.at[a, k], zr.at[a, k], z_peer(k)).wait_recv()
        for j in range(1, ys_count):
            y_copy(a, k, j).start()
        c_copy(a, k, 0).start()

    def forward_c(a, k):
        for j in range(1, ys_count):
            y_wait(a, k, j)
            c_copy(a, k, j).start()

    def ready(a, k):
        for i in range(ys_count):
            c_wait(a, k, i)

    def sent(a):
        for k in range(Z):
            if k > 0:
                z_copy(a, k).wait_send()
            for j in range(1, ys_count):
                y_copy(a, k, j).wait_send()
            for i in range(ys_count):
                c_copy(a, k, i).wait_send()

    own_cols = pl.ds(pl.multiple_of(m * feat, feat), feat)
    dg[pl.ds(0, rows_t), own_cols] = dy_ref[...]
    forward_y(1, 0)

    groups = groups_ref[...]
    onehot = (lax.broadcasted_iota(jnp.int32, (groups_total, nb), 0) == groups).astype(F32)

    def group_sums(values):
        blocks = values.reshape(nb, BLK, feat).sum(axis=1)
        return dot(onehot, blocks, precision=lax.Precision.HIGHEST)

    def per_block(table):
        return dot(onehot, table, 0, 0, precision=lax.Precision.HIGHEST)

    def per_token(blocks):
        wide = jnp.broadcast_to(blocks[:, None, :], (nb, BLK, feat))
        return wide.reshape(rows_t, feat)

    def exchange_start(buf, slot, s, r, count, peer):
        for j in range(1, count):
            remote(buf.at[slot], buf.at[slot], s.at[j], r.at[j], peer(j)).start()

    def exchange_sum(buf, slot, s, r, count, peer):
        for j in range(1, count):
            remote(buf.at[slot], buf.at[slot], s.at[j], r.at[j], peer(j)).wait()
        total = buf[0]
        for j in range(1, count):
            total = total + buf[j]
        return total

    def tok_total(value, bx, bz, xsend, xrecv, zsend, zrecv):
        bx[x] = value
        exchange_start(bx, x, xsend, xrecv, xs, x_peer)
        bz[z] = exchange_sum(bx, x, xsend, xrecv, xs, x_peer)
        exchange_start(bz, z, zsend, zrecv, Z, z_peer)
        return exchange_sum(bz, z, zsend, zrecv, Z, z_peer)

    xf = x_ref[...].astype(F32)
    quad_mean = tok_total(group_sums(xf * xf), stat_x, stat_z, sx_s, sx_r, sz_s, sz_r) / GHOST
    gain = gain_ref[m]
    sblk[...] = per_block(lax.rsqrt(quad_mean + EPSILON))
    normed = x_ref[...].astype(F32) * per_token(sblk[...])
    hg[pl.ds(0, rows_t), own_cols] = (gain * normed).astype(BF16)
    mean_q = jnp.sum(quad_mean, axis=0, keepdims=True) / groups_total
    rn_ref[...] = (1.0 - MOMENTUM) * run_ref[...] + MOMENTUM * mean_q

    forward_y(0, 0)
    for k in range(1, Z):
        z_copy(0, k).start()
    for k in range(1, Z):
        z_copy(1, k).start()
    forward_c(1, 0)
    ready(1, 0)

    tile = min(256, width)
    steps = width // tile

    def cols(n, size):
        return pl.ds(pl.multiple_of(n * size, size), size)

    load_a.wait()
    load_b.wait()
    for k in range(Z):
        forward_c(0, k)
        if k + 1 < Z:
            forward_y(0, k + 1)
        else:
            forward_y(1, 1)
        ready(0, k)
        part = pl.ds(k * rows_t, rows_t)

        def hidden_tile(n, carry):
            w = cols(n, tile)
            gate = dot(hg[part, :], wa[:, w])
            lift = dot(hg[part, :], wb[:, w])
            sigma = 1.0 / (1.0 + jnp.exp(-gate))
            act = gate * sigma
            hidden[part, w] = (act * lift).astype(BF16)
            ggi[part, w] = (lift * sigma * (1.0 + gate * (1.0 - sigma))).astype(BF16)
            gl[part, w] = act.astype(BF16)
            return carry

        lax.fori_loop(0, steps, hidden_tile, 0)

    load_d = pltpu.make_async_copy(wd_hbm, wa, w_sem.at[0])
    load_d.start()

    def transposed(src, dst):
        for j in range(xs):
            first = (z * xs + (x + j) % xs) * rows
            lanes = pl.ds(pl.multiple_of(first, rows), rows)
            for k in range(Z):
                part = pl.ds(k * rows_t, rows_t)
                value = src[part, lanes].astype(F32).T.astype(BF16)
                dst[pl.ds(j * rows, rows), part] = value

    transposed(hg, ht)
    load_d.wait()

    for k in range(Z):
        if k > 0:
            forward_c(1, k)
        if 0 < k < Z - 1:
            forward_y(1, k + 1)
        if k > 0:
            ready(1, k)
        part = pl.ds(k * rows_t, rows_t)

        def gradient_tile(n, carry):
            w = cols(n, tile)
            gh = dot(dg[part, :], wa[:, w])
            ggi[part, w] = (gh * ggi[part, w].astype(F32)).astype(BF16)
            gl[part, w] = (gh * gl[part, w].astype(F32)).astype(BF16)
            return carry

        lax.fori_loop(0, steps, gradient_tile, 0)

    transposed(dg, dt)
    sent(0)
    sent(1)

    big = min(512, width)
    sides = ((ht, ggi), (ht, gl), (dt, hidden))
    other = (xs - 1) * rows

    def rs_copy(w, j):
        src = hg.at[pl.ds((w * (xs - 1) + j - 1) * rows, rows), pl.ds(0, width)]
        return remote(src, rbuf.at[w, j - 1], rs_s.at[w, j], rs_r.at[w, j], x_peer(j))

    def rs_compute(w):
        left, right = sides[w]

        def rs_tile(n, carry):
            lanes = cols(n, big)
            value = dot(left[pl.ds(rows, other), :], right[:, lanes])
            hg[pl.ds(w * other, other), lanes] = value.astype(BF16)
            return carry

        lax.fori_loop(0, width // big, rs_tile, 0)

    def rs_start(w):
        for j in range(1, xs):
            rs_copy(w, j).start()

    rs_compute(0)
    rs_start(0)
    rs_compute(1)
    rs_start(1)

    def m_copy(a, j):
        src = dg.at[pl.ds(a * rows_t, rows_t), pl.ds((j - 1) * feat, feat)]
        return remote(src, mp_recv.at[a, j - 1], ms_s.at[a, j], ms_r.at[a, j], mp_peer(j))

    def over_hidden(a, terms, own):
        def one(j, start):
            first = pl.multiple_of(((m + j) % mp_count) * feat, feat)
            value = None
            for left, weight in terms:
                more = dot(left[pl.ds(0, rows_t), :], weight[pl.ds(first, feat), :], 1, 1)
                value = more if value is None else value + more
            return value

        for j in range(1, mp_count):
            dg[pl.ds(a * rows_t, rows_t), pl.ds((j - 1) * feat, feat)] = one(j, 0).astype(BF16)
            m_copy(a, j).start()
        own[...] = one(0, 0)

    def received(a, own):
        total = own[...]
        for j in range(1, mp_count):
            m_copy(a, j).wait()
            total = total + mp_recv[a, j - 1].astype(F32)
        return total

    over_hidden(0, ((hidden, wa),), own_b)
    load_g = pltpu.make_async_copy(wg_hbm, wa, w_sem.at[0])
    load_g.start()
    rs_compute(2)
    load_g.wait()
    over_hidden(1, ((ggi, wa), (gl, wb)), own_g)
    bo_ref[...] = (x_ref[...].astype(F32) + received(0, own_b)).astype(BF16)
    own_g[...] = received(1, own_g)
    normed = x_ref[...].astype(F32) * per_token(sblk[...])
    part_x[x] = group_sums(own_g[...] * normed)
    exchange_start(part_x, x, px_s, px_r, xs, x_peer)
    rs_start(2)
    part_z[z] = exchange_sum(part_x, x, px_s, px_r, xs, x_peer)
    exchange_start(part_z, z, pz_s, pz_r, Z, z_peer)
    total = exchange_sum(part_z, z, pz_s, pz_r, Z, z_peer)
    gg_ref[...] = jnp.sum(total, axis=0, keepdims=True)
    scale = per_token(sblk[...])
    normed = x_ref[...].astype(F32) * scale
    mean_term = per_token(per_block(gain * total / GHOST))
    gt_ref[...] = (
        dy_ref[...].astype(F32) + scale * (gain * own_g[...] - normed * mean_term)
    ).astype(BF16)

    outs = (dgate_hbm, dup_hbm, ddown_hbm)
    pending = {}
    count = 0
    for w in range(3):
        for j in range(1, xs):
            rs_copy(w, j).wait()
        left, right = sides[w]
        for n in range(width // big):
            slot = count % 2
            if slot in pending:
                pending[slot].wait()
            lanes = pl.ds(n * big, big)
            value = dot(left[pl.ds(0, rows), :], right[:, lanes])
            for j in range(1, xs):
                value = value + rbuf[w, j - 1, :, lanes].astype(F32)
            stage[slot] = value
            copy = pltpu.make_async_copy(stage.at[slot], outs[w].at[:, lanes], o_sem.at[slot])
            copy.start()
            pending[slot] = copy
            count += 1
    for copy in pending.values():
        copy.wait()


def body(tokens, norm_gain, running_sq, gate_weight, up_weight, down_weight_t, groups, cotangent):
    tok_count, mp_count = lax.axis_size("tok"), lax.axis_size("mp")
    rows_t, feat = tokens.shape
    full, width = gate_weight.shape
    xs = tok_count // Z
    rows = full // tok_count
    nb = rows_t // BLK
    groups_total = rows_t * tok_count // GHOST
    ys_count = mp_count // CORES
    big = min(512, width)
    vmem = pl.BlockSpec(memory_space=pltpu.VMEM)
    hbm = pl.BlockSpec(memory_space=pl.ANY)
    dma = pltpu.SemaphoreType.DMA
    table = (groups_total, feat)
    grad = jax.ShapeDtypeStruct((rows, width), F32)
    outs = pl.pallas_call(
        functools.partial(kernel, tok_count, mp_count),
        out_shape=(
            jax.ShapeDtypeStruct((rows_t, feat), BF16),
            jax.ShapeDtypeStruct((rows_t, feat), BF16),
            jax.ShapeDtypeStruct((1, feat), F32),
            jax.ShapeDtypeStruct((1, feat), F32),
            grad,
            grad,
            grad,
        ),
        in_specs=[vmem] * 5 + [hbm] * 3,
        out_specs=(vmem,) * 4 + (hbm,) * 3,
        scratch_shapes=[
            pltpu.VMEM((full, width), BF16),
            pltpu.VMEM((full, width), BF16),
            pltpu.VMEM((Z * rows_t, full), BF16),
            pltpu.VMEM((Z * rows_t, full), BF16),
            pltpu.VMEM((Z * rows_t, width), BF16),
            pltpu.VMEM((Z * rows_t, width), BF16),
            pltpu.VMEM((Z * rows_t, width), BF16),
            pltpu.VMEM((xs * rows, Z * rows_t), BF16),
            pltpu.VMEM((xs * rows, Z * rows_t), BF16),
            pltpu.VMEM((3, xs - 1, rows, width), BF16),
            pltpu.VMEM((2, mp_count - 1, rows_t, feat), BF16),
            pltpu.VMEM((2, rows, big), F32),
            pltpu.VMEM((nb, feat), F32),
            pltpu.VMEM((xs,) + table, F32),
            pltpu.VMEM((Z,) + table, F32),
            pltpu.VMEM((xs,) + table, F32),
            pltpu.VMEM((Z,) + table, F32),
            pltpu.VMEM((rows_t, feat), F32),
            pltpu.VMEM((rows_t, feat), F32),
            dma((2,)),
            dma((2, Z)),
            dma((2, Z)),
            dma((2, Z, ys_count)),
            dma((2, Z, ys_count)),
            dma((2, Z, ys_count)),
            dma((2, Z, ys_count)),
            dma((xs,)),
            dma((xs,)),
            dma((Z,)),
            dma((Z,)),
            dma((xs,)),
            dma((xs,)),
            dma((Z,)),
            dma((Z,)),
            dma((3, xs)),
            dma((3, xs)),
            dma((2, mp_count)),
            dma((2, mp_count)),
            dma((2,)),
        ],
        compiler_params=pltpu.CompilerParams(
            collective_id=0, has_side_effects=True, vmem_limit_bytes=67043328
        ),
        name="sublayer",
    )(
        tokens,
        norm_gain.reshape(mp_count, 1, feat),
        running_sq.reshape(1, feat),
        groups.reshape(1, nb),
        cotangent,
        gate_weight,
        up_weight,
        down_weight_t,
    )
    block_out, grad_tokens, running_new, grad_gain, grad_gate, grad_up, grad_down_t = outs
    return (
        block_out,
        grad_tokens,
        running_new.reshape(feat),
        grad_gain.reshape(feat),
        grad_gate,
        grad_up,
        grad_down_t,
    )


def solution(mesh):
    placed = (
        P("tok", "mp"),
        P(),
        P("mp"),
        P(None, "mp"),
        P(None, "mp"),
        P(None, "mp"),
        P("tok"),
        P("tok", "mp"),
    )
    return jax.shard_map(
        body,
        mesh=mesh,
        in_specs=placed,
        out_specs=(
            P("tok", "mp"),
            P("tok", "mp"),
            P("mp"),
            P("mp"),
            P("tok", "mp"),
            P("tok", "mp"),
            P("tok", "mp"),
        ),
        check_vma=False,
    )
```

profile of v0, /device:TPU:14, one launch (start us, length us, event | category | flops | bytes accessed | tf_op | source)
XLA Modules:
  0.0 211.3 jit_solution(11478553965642487018)
XLA Ops:
  0.6 197.6 %sublayer.1 = (bf16[384,512]{1,0:T(8,128)(2,1)}, bf16[384,512]{1,0:T(8,128)(2,1)}, f32[1,512]{1,0:T(1,128)}, f32[1,512]{1,0:T(1,128)}, f32[256,2048]{1,0:T(8,128...) custom-call(bf16[384,512]{1,0:T(8,128)(2,1)} %x_ref.1, f32[4,1,512]{2,1,0:T(1,128)} %bitcast.5, f32[1,512]{1,0:T(1,128)} %bitcast.6, ...), custom_call_target="tpu_custom_call" | custom-call | tf_op jit(solution)/shard_map/sublayer/pallas_call | solution.py:424
  198.3 1.8 copy.22
  200.0 1.8 copy.23
  201.8 1.3 copy.24
  203.1 1.3 copy.25
  204.3 0.0 copy-start.1
  204.3 3.3 %copy.26 = f32[256,2048]{1,0:T(8,128)} copy(f32[256,2048]{1,0:T(8,128)} %get-tuple-element.32) | data formatting | bytes 4194304
  207.6 0.0 copy-done.1
  207.6 0.0 copy-start
  207.6 1.3 copy.27
  208.9 1.0 copy-done
  210.0 1.3 copy.28
Async XLA Ops:
  204.3 3.3 %copy-start.1 = (f32[256,2048]{1,0:T(8,128)S(1)}, f32[256,2048]{1,0:T(8,128)}, u32[]{:S(2)}) copy-start(f32[256,2048]{1,0:T(8,128)} %get-tuple-element.33) | copy-start | bytes 6291460
  207.6 2.3 %copy-start = (f32[256,2048]{1,0:T(8,128)S(1)}, f32[256,2048]{1,0:T(8,128)}, u32[]{:S(2)}) copy-start(f32[256,2048]{1,0:T(8,128)} %get-tuple-element.34) | copy-start | bytes 6291460
where the time goes:
time: 212 us; the launch traced here: 211 us
  Pallas kernels  198 us (93%)
  local copies, waits for them, and re-layouts  13 us (6%)
    pallas_call x1, Pallas kernels, body(): pl.pallas_call(functools.partial(kernel, tok_count, mp_count), out_shape=...  198 us
    unnamed x11, local copies, waits for them, and re-layouts  13 us

commit v1 on v0

--- a/solution.py
+++ b/solution.py
@@ -39,9 +39,8 @@
     gt_ref,
     rn_ref,
     gg_ref,
-    dgate_hbm,
-    dup_hbm,
-    ddown_hbm,
+    own_hbm,
+    recv_hbm,
     wa,
     wb,
     hg,
@@ -51,7 +50,6 @@
     gl,
     ht,
     dt,
-    rbuf,
     mp_recv,
     stage,
     sblk,
@@ -96,6 +94,8 @@
     z, x = me // xs, me % xs
     y, c = m // CORES, m % CORES
 
+    inner = (z == 1) | (z == 2)
+
     def z_peer(k):
         zz = z + 0
         if k & 1:
@@ -138,8 +138,58 @@
         col = pl.multiple_of(owner * feat, feat)
         return bufs[a].at[pl.ds(k * rows_t, rows_t), pl.ds(col, feat)]
 
-    def z_copy(a, k):
-        return remote(block(a, 0, m), block(a, k, m), zs.at[a, k], zr.at[a, k], z_peer(k))
+    to_near, to_mid, near_to_mid, mid_to_near, far_to_near = (
+        (0, 0, 1, 1), (1, 0, 3, 3), (2, 1, 2, 3), (3, 3, 2, 1), (4, 2, 3, 1)
+    )
+
+    def z_copy(a, hop):
+        slot, held, there, k = hop
+        return remote(
+            block(a, held, m), block(a, there, m), zs.at[a, slot], zr.at[a, there], z_peer(k)
+        )
+
+    def z_wait(a, k):
+        b = block(a, k, m)
+        remote(b, b, zs.at[a, 0], zr.at[a, k], z_peer(1)).wait_recv()
+
+    def z_own(a):
+        z_copy(a, to_near).start()
+
+        @pl.when(inner)
+        def _():
+            z_copy(a, to_mid).start()
+
+    def z_first(a):
+        z_wait(a, 1)
+
+        @pl.when(inner)
+        def _():
+            z_copy(a, near_to_mid).start()
+
+        forward_y(a, 1)
+
+        @pl.when(inner)
+        def _():
+            z_wait(a, 3)
+            z_copy(a, mid_to_near).start()
+            forward_y(a, 3)
+
+    def z_second(a):
+        z_wait(a, 2)
+
+        @pl.when(inner)
+        def _():
+            z_copy(a, far_to_near).start()
+
+        forward_y(a, 2)
+
+    outer = jnp.logical_not(inner)
+
+    def z_third(a):
+        @pl.when(outer)
+        def _():
+            z_wait(a, 3)
+            forward_y(a, 3)
 
     def y_copy(a, k, j):
         return remote(block(a, k, m), block(a, k, m), ys.at[a, k, j], yr.at[a, k, j], y_peer(j))
@@ -160,30 +210,71 @@
         remote(b, b, cs.at[a, k, i], cr.at[a, k, i], core_peer).wait_recv()
 
     def forward_y(a, k):
-        if k > 0:
-            b = block(a, k, m)
-            remote(b, b, zs.at[a, k], zr.at[a, k], z_peer(k)).wait_recv()
         for j in range(1, ys_count):
             y_copy(a, k, j).start()
         c_copy(a, k, 0).start()
 
-    def forward_c(a, k):
+    def wanted(owner, at=z):
+        return (owner * feat) // (xs * rows) == at
+
+    def holds(at):
+        return (at * xs * rows) // (feat * CORES) == y
+
+    near = z + 1 - 2 * (z % 2)
+    first_out = wanted(m)
+    alone = jnp.logical_not(holds(z))
+    early = first_out | alone
+    late = jnp.logical_not(early)
+    near_late = holds(near) & jnp.logical_not(wanted(m, near))
+    near_early = jnp.logical_not(near_late)
+
+    def take(k):
+        z_wait(1, k)
+        forward_y(1, k)
+
+    def forward_c(a, k, choose=None):
         for j in range(1, ys_count):
-            y_wait(a, k, j)
-            c_copy(a, k, j).start()
-
-    def ready(a, k):
+
+            def go(j=j):
+                y_wait(a, k, j)
+                c_copy(a, k, j).start()
+
+            if choose is None:
+                go()
+            else:
+                pl.when(wanted(y_from(j)) == choose)(go)
+
+    def ready(a, k, choose=None):
         for i in range(ys_count):
-            c_wait(a, k, i)
-
-    def sent(a):
-        for k in range(Z):
-            if k > 0:
-                z_copy(a, k).wait_send()
-            for j in range(1, ys_count):
-                y_copy(a, k, j).wait_send()
-            for i in range(ys_count):
-                c_copy(a, k, i).wait_send()
+            owner = ((y + ys_count - i) % ys_count) * CORES + (1 - c)
+            if choose is None:
+                c_wait(a, k, i)
+            else:
+                pl.when(wanted(owner) == choose)(functools.partial(c_wait, a, k, i))
+
+    def chunk_sent(a, k):
+        for j in range(1, ys_count):
+            y_copy(a, k, j).wait_send()
+        for i in range(ys_count):
+            c_copy(a, k, i).wait_send()
+
+    def own_sent(a):
+        z_copy(a, to_near).wait_send()
+
+        @pl.when(inner)
+        def _():
+            z_copy(a, to_mid).wait_send()
+
+        chunk_sent(a, 0)
+
+    def rest_sent(a):
+        @pl.when(inner)
+        def _():
+            for which in (near_to_mid, mid_to_near, far_to_near):
+                z_copy(a, which).wait_send()
+
+        for k in range(1, Z):
+            chunk_sent(a, k)
 
     own_cols = pl.ds(pl.multiple_of(m * feat, feat), feat)
     dg[pl.ds(0, rows_t), own_cols] = dy_ref[...]
@@ -231,29 +322,18 @@
     mean_q = jnp.sum(quad_mean, axis=0, keepdims=True) / groups_total
     rn_ref[...] = (1.0 - MOMENTUM) * run_ref[...] + MOMENTUM * mean_q
 
+    z_own(0)
     forward_y(0, 0)
-    for k in range(1, Z):
-        z_copy(0, k).start()
-    for k in range(1, Z):
-        z_copy(1, k).start()
     forward_c(1, 0)
     ready(1, 0)
 
-    tile = min(256, width)
+    tile = min(512, width // 2)
     steps = width // tile
 
     def cols(n, size):
         return pl.ds(pl.multiple_of(n * size, size), size)
 
-    load_a.wait()
-    load_b.wait()
-    for k in range(Z):
-        forward_c(0, k)
-        if k + 1 < Z:
-            forward_y(0, k + 1)
-        else:
-            forward_y(1, 1)
-        ready(0, k)
+    def hidden_half(k, first, last):
         part = pl.ds(k * rows_t, rows_t)
 
         def hidden_tile(n, carry):
@@ -267,7 +347,62 @@
             gl[part, w] = act.astype(BF16)
             return carry
 
-        lax.fori_loop(0, steps, hidden_tile, 0)
+        lax.fori_loop(first, last, hidden_tile, 0)
+
+    def at_once(flag, *calls):
+        @pl.when(flag)
+        def _():
+            for call, arg in calls:
+                call(arg)
+
+    def hop(which):
+        z_copy(1, which).start()
+
+    def hold(k):
+        z_wait(1, k)
+
+    def pass_on(k):
+        forward_y(1, k)
+
+    load_a.wait()
+    load_b.wait()
+    forward_c(0, 0)
+    z_first(0)
+    at_once(outer, (hop, to_near))
+    at_once(inner, (hop, to_mid))
+    ready(0, 0)
+    hidden_half(0, 0, steps)
+    z_second(0)
+    at_once(inner & near_early, (hop, to_near))
+    forward_c(0, 1)
+    ready(0, 1)
+    hidden_half(1, 0, steps)
+    z_third(0)
+    at_once(inner, (hold, 1), (hop, near_to_mid), (hold, 3))
+    at_once(inner & near_early, (hop, mid_to_near))
+    at_once(inner & near_late, (hop, to_near))
+    at_once(inner & early, (pass_on, 1), (pass_on, 3))
+    forward_c(0, 2)
+    ready(0, 2)
+    hidden_half(2, 0, steps // 2)
+    at_once(inner, (hold, 2))
+    at_once(inner & near_early, (hop, far_to_near))
+    at_once(inner & near_late, (hop, mid_to_near))
+    at_once(inner & early, (pass_on, 2))
+    at_once(outer & early, (take, 1))
+    hidden_half(2, steps // 2, steps)
+    at_once(inner & near_late, (hop, far_to_near))
+    forward_c(0, 3)
+    at_once(outer & early, (take, 2))
+    at_once(inner & late, (pass_on, 1), (pass_on, 3))
+    ready(0, 3)
+    at_once(outer & late, (take, 1))
+    hidden_half(3, 0, steps // 2)
+    at_once(outer & early, (take, 3))
+    at_once(inner & late, (pass_on, 2))
+    at_once(outer & late, (take, 2))
+    hidden_half(3, steps // 2, steps)
+    at_once(outer & late, (take, 3))
 
     load_d = pltpu.make_async_copy(wd_hbm, wa, w_sem.at[0])
     load_d.start()
@@ -282,15 +417,90 @@
                 dst[pl.ds(j * rows, rows), part] = value
 
     transposed(hg, ht)
+    for k in range(1, Z):
+        forward_c(1, k, True)
+    for k in range(1, Z):
+        ready(1, k, True)
+    transposed(dg, dt)
+    own_sent(0)
+    rest_sent(0)
+
+    big = min(512, width // 2)
+    sides = ((ht, ggi), (ht, gl), (dt, hidden))
+    other = (xs - 1) * rows
+    halves = 2
+    half = width // halves
+
+    def rs_copy(w, j, h):
+        lanes = pl.ds(h * half, half)
+        src = hg.at[pl.ds((w * (xs - 1) + j - 1) * rows, rows), lanes]
+        dst = recv_hbm.at[w, j - 1, :, lanes]
+        return remote(src, dst, rs_s.at[w, j, h], rs_r.at[w, j, h], x_peer(j))
+
+    def rs_compute(w, h):
+        left, right = sides[w]
+        each = half // big
+
+        def rs_tile(n, carry):
+            lanes = cols(n, big)
+            value = dot(left[pl.ds(rows, other), :], right[:, lanes])
+            hg[pl.ds(w * other, other), lanes] = value.astype(BF16)
+            return carry
+
+        lax.fori_loop(h * each, (h + 1) * each, rs_tile, 0)
+
+    def rs_start(w, h):
+        for j in range(1, xs):
+            rs_copy(w, j, h).start()
+
+    def m_copy(a, j):
+        src = dg.at[pl.ds(a * rows_t, rows_t), pl.ds((j - 1) * feat, feat)]
+        return remote(src, mp_recv.at[a, j - 1], ms_s.at[a, j], ms_r.at[a, j], mp_peer(j))
+
+    def over_hidden(a, terms, own, send):
+        def one(j):
+            first = pl.multiple_of(((m + j) % mp_count) * feat, feat)
+            value = None
+            for left, weight in terms:
+                more = dot(left[pl.ds(0, rows_t), :], weight[pl.ds(first, feat), :], 1, 1)
+                value = more if value is None else value + more
+            return value
+
+        for j in range(1, mp_count):
+            dg[pl.ds(a * rows_t, rows_t), pl.ds((j - 1) * feat, feat)] = one(j).astype(BF16)
+            if send:
+                m_copy(a, j).start()
+        own[...] = one(0)
+
+    def received(a, own):
+        total = own[...]
+        for j in range(1, mp_count):
+            m_copy(a, j).wait()
+            total = total + mp_recv[a, j - 1].astype(F32)
+        return total
+
+    pending = {}
+    turn = [0]
+
+    def own_rows(w):
+        left, right = sides[w]
+        for n in range(width // big):
+            slot = turn[0] % 2
+            if slot in pending:
+                pending[slot].wait()
+            lanes = pl.ds(n * big, big)
+            stage[slot] = dot(left[pl.ds(0, rows), :], right[:, lanes])
+            copy = pltpu.make_async_copy(stage.at[slot], own_hbm.at[w, :, lanes], o_sem.at[slot])
+            copy.start()
+            pending[slot] = copy
+            turn[0] += 1
+
+    for h in range(halves):
+        rs_compute(2, h)
+        rs_start(2, h)
     load_d.wait()
 
-    for k in range(Z):
-        if k > 0:
-            forward_c(1, k)
-        if 0 < k < Z - 1:
-            forward_y(1, k + 1)
-        if k > 0:
-            ready(1, k)
+    def gradient_part(k, first, last):
         part = pl.ds(k * rows_t, rows_t)
 
         def gradient_tile(n, carry):
@@ -300,77 +510,44 @@
             gl[part, w] = (gh * gl[part, w].astype(F32)).astype(BF16)
             return carry
 
-        lax.fori_loop(0, steps, gradient_tile, 0)
-
-    transposed(dg, dt)
-    sent(0)
-    sent(1)
-
-    big = min(512, width)
-    sides = ((ht, ggi), (ht, gl), (dt, hidden))
-    other = (xs - 1) * rows
-
-    def rs_copy(w, j):
-        src = hg.at[pl.ds((w * (xs - 1) + j - 1) * rows, rows), pl.ds(0, width)]
-        return remote(src, rbuf.at[w, j - 1], rs_s.at[w, j], rs_r.at[w, j], x_peer(j))
-
-    def rs_compute(w):
-        left, right = sides[w]
-
-        def rs_tile(n, carry):
-            lanes = cols(n, big)
-            value = dot(left[pl.ds(rows, other), :], right[:, lanes])
-            hg[pl.ds(w * other, other), lanes] = value.astype(BF16)
-            return carry
-
-        lax.fori_loop(0, width // big, rs_tile, 0)
-
-    def rs_start(w):
-        for j in range(1, xs):
-            rs_copy(w, j).start()
-
-    rs_compute(0)
-    rs_start(0)
-    rs_compute(1)
-    rs_start(1)
-
-    def m_copy(a, j):
-        src = dg.at[pl.ds(a * rows_t, rows_t), pl.ds((j - 1) * feat, feat)]
-        return remote(src, mp_recv.at[a, j - 1], ms_s.at[a, j], ms_r.at[a, j], mp_peer(j))
-
-    def over_hidden(a, terms, own):
-        def one(j, start):
-            first = pl.multiple_of(((m + j) % mp_count) * feat, feat)
-            value = None
-            for left, weight in terms:
-                more = dot(left[pl.ds(0, rows_t), :], weight[pl.ds(first, feat), :], 1, 1)
-                value = more if value is None else value + more
-            return value
-
-        for j in range(1, mp_count):
-            dg[pl.ds(a * rows_t, rows_t), pl.ds((j - 1) * feat, feat)] = one(j, 0).astype(BF16)
-            m_copy(a, j).start()
-        own[...] = one(0, 0)
-
-    def received(a, own):
-        total = own[...]
-        for j in range(1, mp_count):
-            m_copy(a, j).wait()
-            total = total + mp_recv[a, j - 1].astype(F32)
-        return total
-
-    over_hidden(0, ((hidden, wa),), own_b)
+        lax.fori_loop(first, last, gradient_tile, 0)
+
+    forward_c(1, 1, False)
+    gradient_part(0, 0, steps)
+    forward_c(1, 2, False)
+    own_sent(1)
+    over_hidden(0, ((hidden, wa),), own_b, False)
+    ready(1, 1, False)
+    gradient_part(1, 0, steps)
+    forward_c(1, 3, False)
+    ready(1, 2, False)
+    gradient_part(2, 0, steps)
+    ready(1, 3, False)
+    gradient_part(Z - 1, 0, steps // 2)
+    rs_compute(0, 0)
+    rs_start(0, 0)
+    gradient_part(Z - 1, steps // 2, steps)
     load_g = pltpu.make_async_copy(wg_hbm, wa, w_sem.at[0])
     load_g.start()
-    rs_compute(2)
+    rs_compute(1, 0)
+    rs_start(1, 0)
+    rs_compute(0, 1)
+    rs_start(0, 1)
+    rs_compute(1, 1)
+    rest_sent(1)
     load_g.wait()
-    over_hidden(1, ((ggi, wa), (gl, wb)), own_g)
-    bo_ref[...] = (x_ref[...].astype(F32) + received(0, own_b)).astype(BF16)
+    over_hidden(1, ((ggi, wa), (gl, wb)), own_g, True)
+    for j in range(1, mp_count):
+        m_copy(0, j).start()
+    for w in range(3):
+        own_rows(w)
+    for copy in pending.values():
+        copy.wait()
     own_g[...] = received(1, own_g)
     normed = x_ref[...].astype(F32) * per_token(sblk[...])
     part_x[x] = group_sums(own_g[...] * normed)
     exchange_start(part_x, x, px_s, px_r, xs, x_peer)
-    rs_start(2)
+    rs_start(1, 1)
     part_z[z] = exchange_sum(part_x, x, px_s, px_r, xs, x_peer)
     exchange_start(part_z, z, pz_s, pz_r, Z, z_peer)
     total = exchange_sum(part_z, z, pz_s, pz_r, Z, z_peer)
@@ -381,29 +558,26 @@
     gt_ref[...] = (
         dy_ref[...].astype(F32) + scale * (gain * own_g[...] - normed * mean_term)
     ).astype(BF16)
-
-    outs = (dgate_hbm, dup_hbm, ddown_hbm)
-    pending = {}
-    count = 0
+    bo_ref[...] = (x_ref[...].astype(F32) + received(0, own_b)).astype(BF16)
     for w in range(3):
         for j in range(1, xs):
-            rs_copy(w, j).wait()
-        left, right = sides[w]
-        for n in range(width // big):
-            slot = count % 2
-            if slot in pending:
-                pending[slot].wait()
-            lanes = pl.ds(n * big, big)
-            value = dot(left[pl.ds(0, rows), :], right[:, lanes])
-            for j in range(1, xs):
-                value = value + rbuf[w, j - 1, :, lanes].astype(F32)
-            stage[slot] = value
-            copy = pltpu.make_async_copy(stage.at[slot], outs[w].at[:, lanes], o_sem.at[slot])
-            copy.start()
-            pending[slot] = copy
-            count += 1
-    for copy in pending.values():
-        copy.wait()
+            for h in range(halves):
+                rs_copy(w, j, h).wait()
+
+
+def finish(own, recv, bo, gt, rn, gg, bo_out, gt_out, rn_out, gg_out, dgate, dup, ddown):
+    for w, out in enumerate((dgate, dup, ddown)):
+        value = own[w]
+        for j in range(recv.shape[1]):
+            value = value + recv[w, j].astype(F32)
+        out[...] = value
+
+    @pl.when(pl.program_id(0) == 0)
+    def _():
+        bo_out[...] = bo[...]
+        gt_out[...] = gt[...]
+        rn_out[...] = rn[...]
+        gg_out[...] = gg[...]
 
 
 def body(tokens, norm_gain, running_sq, gate_weight, up_weight, down_weight_t, groups, cotangent):
@@ -415,25 +589,26 @@
     nb = rows_t // BLK
     groups_total = rows_t * tok_count // GHOST
     ys_count = mp_count // CORES
-    big = min(512, width)
+    big = min(512, width // 2)
     vmem = pl.BlockSpec(memory_space=pltpu.VMEM)
     hbm = pl.BlockSpec(memory_space=pl.ANY)
     dma = pltpu.SemaphoreType.DMA
     table = (groups_total, feat)
-    grad = jax.ShapeDtypeStruct((rows, width), F32)
+    small = (
+        jax.ShapeDtypeStruct((rows_t, feat), BF16),
+        jax.ShapeDtypeStruct((rows_t, feat), BF16),
+        jax.ShapeDtypeStruct((1, feat), F32),
+        jax.ShapeDtypeStruct((1, feat), F32),
+    )
     outs = pl.pallas_call(
         functools.partial(kernel, tok_count, mp_count),
-        out_shape=(
-            jax.ShapeDtypeStruct((rows_t, feat), BF16),
-            jax.ShapeDtypeStruct((rows_t, feat), BF16),
-            jax.ShapeDtypeStruct((1, feat), F32),
-            jax.ShapeDtypeStruct((1, feat), F32),
-            grad,
-            grad,
-            grad,
+        out_shape=small
+        + (
+            jax.ShapeDtypeStruct((3, rows, width), F32),
+            jax.ShapeDtypeStruct((3, xs - 1, rows, width), BF16),
         ),
         in_specs=[vmem] * 5 + [hbm] * 3,
-        out_specs=(vmem,) * 4 + (hbm,) * 3,
+        out_specs=(vmem,) * 4 + (hbm,) * 2,
         scratch_shapes=[
             pltpu.VMEM((full, width), BF16),
             pltpu.VMEM((full, width), BF16),
@@ -444,7 +619,6 @@
             pltpu.VMEM((Z * rows_t, width), BF16),
             pltpu.VMEM((xs * rows, Z * rows_t), BF16),
             pltpu.VMEM((xs * rows, Z * rows_t), BF16),
-            pltpu.VMEM((3, xs - 1, rows, width), BF16),
             pltpu.VMEM((2, mp_count - 1, rows_t, feat), BF16),
             pltpu.VMEM((2, rows, big), F32),
             pltpu.VMEM((nb, feat), F32),
@@ -455,7 +629,7 @@
             pltpu.VMEM((rows_t, feat), F32),
             pltpu.VMEM((rows_t, feat), F32),
             dma((2,)),
-            dma((2, Z)),
+            dma((2, 5)),
             dma((2, Z)),
             dma((2, Z, ys_count)),
             dma((2, Z, ys_count)),
@@ -469,8 +643,8 @@
             dma((xs,)),
             dma((Z,)),
             dma((Z,)),
-            dma((3, xs)),
-            dma((3, xs)),
+            dma((3, xs, 2)),
+            dma((3, xs, 2)),
             dma((2, mp_count)),
             dma((2, mp_count)),
             dma((2,)),
@@ -489,7 +663,22 @@
         up_weight,
         down_weight_t,
     )
-    block_out, grad_tokens, running_new, grad_gain, grad_gate, grad_up, grad_down_t = outs
+    block_out, grad_tokens, running_new, grad_gain, own, recv = outs
+    span = min(512, width)
+    whole = [pl.BlockSpec(leaf.shape, lambda n: (0, 0)) for leaf in small]
+    grad = jax.ShapeDtypeStruct((rows, width), F32)
+    block_out, grad_tokens, running_new, grad_gain, grad_gate, grad_up, grad_down_t = pl.pallas_call(
+        finish,
+        grid=(width // span,),
+        out_shape=small + (grad,) * 3,
+        in_specs=[
+            pl.BlockSpec((3, rows, span), lambda n: (0, 0, n)),
+            pl.BlockSpec((3, xs - 1, rows, span), lambda n: (0, 0, 0, n)),
+        ]
+        + whole,
+        out_specs=whole + [pl.BlockSpec((rows, span), lambda n: (0, n))] * 3,
+        name="finish",
+    )(own, recv, block_out, grad_tokens, running_new, grad_gain)
     return (
         block_out,
         grad_tokens,

time: 212 us -> 158 us (0.75)
  the two profiles are of different devices: /device:TPU:14 before, /device:TPU:0 now
where the time goes in v1:
time: 158 us
  Pallas kernels  157 us (99%)
    pallas_call x1, Pallas kernels, body(): pl.pallas_call(functools.partial(kernel, tok_count, mp_count), out_shape=...  150 us
    pallas_call x1, Pallas kernels, body(): pl.pallas_call(finish, grid=(width // span,), out_shape=small + (grad,) *...  7.07 us

profile of v1, /device:TPU:0, one launch (start us, length us, event | category | flops | bytes accessed | tf_op | source)
XLA Modules:
  0.0 157.5 jit_solution(10637537955603106635)
XLA Ops:
  0.6 149.8 %sublayer.1 = (bf16[384,512]{1,0:T(8,128)(2,1)}, bf16[384,512]{1,0:T(8,128)(2,1)}, f32[1,512]{1,0:T(1,128)}, f32[1,512]{1,0:T(1,128)}, f32[3,256,2048]{2,1,0:T(8,128)}, /*index=5*/bf16[3,1,256,2048]{3,2,1,0:T(8,128)(2,1)}) custom-call(bf16[384,512]{1,0:T(8,128)(2,1)} %x_ref.1, f32[4,1,512]{2,1,0:T(1,128)} %bitcast.5, f32[1,512]{1,0:T(1,128)} %bitcast.6, ...), custom_call_target="tpu_custom_call" | custom-call | tf_op jit(solution)/shard_map/sublayer/pallas_call | solution.py:603
  150.4 7.1 %finish.1 = (bf16[384,512]{1,0:T(8,128)(2,1)}, bf16[384,512]{1,0:T(8,128)(2,1)}, f32[1,512]{1,0:T(1,128)}, f32[1,512]{1,0:T(1,128)}, f32[256,2048]{1,0:T(8,128)}...) custom-call(f32[3,256,2048]{2,1,0:T(8,128)} %get-tuple-element.20.own, bf16[3,1,256,2048]{3,2,1,0:T(8,128)(2,1)} %get-tuple-element.21.recv, ...), custom_call_target="tpu_custom_call" | custom-call | tf_op jit(solution)/shard_map/finish/pallas_call | solution.py:670

commit v2 on v1

--- a/solution.py
+++ b/solution.py
@@ -148,7 +148,24 @@
             block(a, held, m), block(a, there, m), zs.at[a, slot], zr.at[a, there], z_peer(k)
         )
 
+    piece = rows_t // 2
+
+    def early_copy(i):
+        col = pl.ds(pl.multiple_of(m * feat, feat), feat)
+        src = dg.at[pl.ds(i * piece, piece), col]
+        dst = dg.at[pl.ds(rows_t + i * piece, piece), col]
+        return remote(src, dst, zs.at[1, 5 * i], zr.at[1, 1 + (Z - 1) * i], z_peer(1))
+
+    def early_wait(i):
+        col = pl.ds(pl.multiple_of(m * feat, feat), feat)
+        b = dg.at[pl.ds(rows_t + i * piece, piece), col]
+        remote(b, b, zs.at[1, 5 * i], zr.at[1, 1 + (Z - 1) * i], z_peer(1)).wait_recv()
+
     def z_wait(a, k):
+        if a == 1 and k == 1:
+            early_wait(0)
+            early_wait(1)
+            return
         b = block(a, k, m)
         remote(b, b, zs.at[a, 0], zr.at[a, k], z_peer(1)).wait_recv()
 
@@ -172,7 +189,6 @@
         def _():
             z_wait(a, 3)
             z_copy(a, mid_to_near).start()
-            forward_y(a, 3)
 
     def z_second(a):
         z_wait(a, 2)
@@ -189,7 +205,8 @@
         @pl.when(outer)
         def _():
             z_wait(a, 3)
-            forward_y(a, 3)
+
+        forward_y(a, 3)
 
     def y_copy(a, k, j):
         return remote(block(a, k, m), block(a, k, m), ys.at[a, k, j], yr.at[a, k, j], y_peer(j))
@@ -220,11 +237,11 @@
     def holds(at):
         return (at * xs * rows) // (feat * CORES) == y
 
-    near = z + 1 - 2 * (z % 2)
     first_out = wanted(m)
     alone = jnp.logical_not(holds(z))
     early = first_out | alone
     late = jnp.logical_not(early)
+    near = z + 1 - 2 * (z % 2)
     near_late = holds(near) & jnp.logical_not(wanted(m, near))
     near_early = jnp.logical_not(near_late)
 
@@ -259,7 +276,11 @@
             c_copy(a, k, i).wait_send()
 
     def own_sent(a):
-        z_copy(a, to_near).wait_send()
+        if a == 1:
+            early_copy(0).wait_send()
+            early_copy(1).wait_send()
+        else:
+            z_copy(a, to_near).wait_send()
 
         @pl.when(inner)
         def _():
@@ -278,6 +299,7 @@
 
     own_cols = pl.ds(pl.multiple_of(m * feat, feat), feat)
     dg[pl.ds(0, rows_t), own_cols] = dy_ref[...]
+    early_copy(0).start()
     forward_y(1, 0)
 
     groups = groups_ref[...]
@@ -306,15 +328,13 @@
             total = total + buf[j]
         return total
 
-    def tok_total(value, bx, bz, xsend, xrecv, zsend, zrecv):
-        bx[x] = value
-        exchange_start(bx, x, xsend, xrecv, xs, x_peer)
-        bz[z] = exchange_sum(bx, x, xsend, xrecv, xs, x_peer)
-        exchange_start(bz, z, zsend, zrecv, Z, z_peer)
-        return exchange_sum(bz, z, zsend, zrecv, Z, z_peer)
-
     xf = x_ref[...].astype(F32)
-    quad_mean = tok_total(group_sums(xf * xf), stat_x, stat_z, sx_s, sx_r, sz_s, sz_r) / GHOST
+    stat_x[x] = group_sums(xf * xf)
+    exchange_start(stat_x, x, sx_s, sx_r, xs, x_peer)
+    stat_z[z] = exchange_sum(stat_x, x, sx_s, sx_r, xs, x_peer)
+    exchange_start(stat_z, z, sz_s, sz_r, Z, z_peer)
+    early_copy(1).start()
+    quad_mean = exchange_sum(stat_z, z, sz_s, sz_r, Z, z_peer) / GHOST
     gain = gain_ref[m]
     sblk[...] = per_block(lax.rsqrt(quad_mean + EPSILON))
     normed = x_ref[...].astype(F32) * per_token(sblk[...])
@@ -364,49 +384,6 @@
     def pass_on(k):
         forward_y(1, k)
 
-    load_a.wait()
-    load_b.wait()
-    forward_c(0, 0)
-    z_first(0)
-    at_once(outer, (hop, to_near))
-    at_once(inner, (hop, to_mid))
-    ready(0, 0)
-    hidden_half(0, 0, steps)
-    z_second(0)
-    at_once(inner & near_early, (hop, to_near))
-    forward_c(0, 1)
-    ready(0, 1)
-    hidden_half(1, 0, steps)
-    z_third(0)
-    at_once(inner, (hold, 1), (hop, near_to_mid), (hold, 3))
-    at_once(inner & near_early, (hop, mid_to_near))
-    at_once(inner & near_late, (hop, to_near))
-    at_once(inner & early, (pass_on, 1), (pass_on, 3))
-    forward_c(0, 2)
-    ready(0, 2)
-    hidden_half(2, 0, steps // 2)
-    at_once(inner, (hold, 2))
-    at_once(inner & near_early, (hop, far_to_near))
-    at_once(inner & near_late, (hop, mid_to_near))
-    at_once(inner & early, (pass_on, 2))
-    at_once(outer & early, (take, 1))
-    hidden_half(2, steps // 2, steps)
-    at_once(inner & near_late, (hop, far_to_near))
-    forward_c(0, 3)
-    at_once(outer & early, (take, 2))
-    at_once(inner & late, (pass_on, 1), (pass_on, 3))
-    ready(0, 3)
-    at_once(outer & late, (take, 1))
-    hidden_half(3, 0, steps // 2)
-    at_once(outer & early, (take, 3))
-    at_once(inner & late, (pass_on, 2))
-    at_once(outer & late, (take, 2))
-    hidden_half(3, steps // 2, steps)
-    at_once(outer & late, (take, 3))
-
-    load_d = pltpu.make_async_copy(wd_hbm, wa, w_sem.at[0])
-    load_d.start()
-
     def transposed(src, dst):
         for j in range(xs):
             first = (z * xs + (x + j) % xs) * rows
@@ -416,14 +393,40 @@
                 value = src[part, lanes].astype(F32).T.astype(BF16)
                 dst[pl.ds(j * rows, rows), part] = value
 
-    transposed(hg, ht)
-    for k in range(1, Z):
-        forward_c(1, k, True)
-    for k in range(1, Z):
-        ready(1, k, True)
-    transposed(dg, dt)
-    own_sent(0)
-    rest_sent(0)
+    at_once(first_out, (take, 1))
+    load_a.wait()
+    load_b.wait()
+    forward_c(0, 0)
+    z_first(0)
+    at_once(inner & first_out, (hop, to_mid), (hop, near_to_mid))
+    at_once(inner & jnp.logical_not(first_out), (hop, to_mid), (hold, 1), (hop, near_to_mid))
+    ready(0, 0)
+    hidden_half(0, 0, steps)
+    z_second(0)
+    forward_c(0, 1)
+    ready(0, 1)
+    hidden_half(1, 0, steps)
+    z_third(0)
+    at_once(inner, (hold, 3))
+    at_once(inner & near_early, (hop, mid_to_near))
+    at_once(inner & first_out, (pass_on, 3))
+    at_once(inner & alone, (pass_on, 1), (pass_on, 3))
+    at_once(outer & jnp.logical_not(first_out), (take, 1))
+    forward_c(0, 2)
+    ready(0, 2)
+    hidden_half(2, 0, steps // 2)
+    at_once(inner, (hold, 2))
+    at_once(inner & near_early, (hop, far_to_near))
+    at_once(inner & near_late, (hop, mid_to_near))
+    at_once(inner & early, (pass_on, 2))
+    hidden_half(2, steps // 2, steps)
+    at_once(inner & near_late, (hop, far_to_near))
+    forward_c(0, 3)
+    at_once(outer & early, (take, 2))
+    ready(0, 3)
+    hidden_half(3, 0, steps // 2)
+    at_once(outer & first_out, (take, 3))
+    at_once(inner & late, (pass_on, 1), (pass_on, 3))
 
     big = min(512, width // 2)
     sides = ((ht, ggi), (ht, gl), (dt, hidden))
@@ -453,31 +456,56 @@
         for j in range(1, xs):
             rs_copy(w, j, h).start()
 
-    def m_copy(a, j):
+    def m_copy(a, j, dev):
         src = dg.at[pl.ds(a * rows_t, rows_t), pl.ds((j - 1) * feat, feat)]
-        return remote(src, mp_recv.at[a, j - 1], ms_s.at[a, j], ms_r.at[a, j], mp_peer(j))
-
-    def over_hidden(a, terms, own, send):
-        def one(j):
-            first = pl.multiple_of(((m + j) % mp_count) * feat, feat)
+        return remote(src, mp_recv.at[a, j - 1], ms_s.at[a, j], ms_r.at[a, j], dev)
+
+    def to_core(a, i):
+        return m_copy(a, 1 + i, core_peer)
+
+    def to_row(a, i):
+        return m_copy(a, ys_count + i, y_peer(i))
+
+    def row_share(a, i, value):
+        to_core(a, i).wait_recv()
+        value = value + mp_recv[a, i].astype(F32)
+        first = (ys_count + i - 1) * feat
+        dg[pl.ds(a * rows_t, rows_t), pl.ds(first, feat)] = value.astype(BF16)
+        to_row(a, i).start()
+
+    def over_hidden(a, terms, keep):
+        def one(i, core):
+            owner = ((y + i) % ys_count) * CORES + core
+            first = pl.multiple_of(owner * feat, feat)
             value = None
             for left, weight in terms:
                 more = dot(left[pl.ds(0, rows_t), :], weight[pl.ds(first, feat), :], 1, 1)
                 value = more if value is None else value + more
             return value
 
-        for j in range(1, mp_count):
-            dg[pl.ds(a * rows_t, rows_t), pl.ds((j - 1) * feat, feat)] = one(j).astype(BF16)
-            if send:
-                m_copy(a, j).start()
-        own[...] = one(0)
+        order = list(range(1, ys_count)) + [0]
+        for i in order:
+            dg[pl.ds(a * rows_t, rows_t), pl.ds(i * feat, feat)] = one(i, 1 - c).astype(BF16)
+            to_core(a, i).start()
+        for i in order:
+            if i == 0 or a == 0:
+                keep[i if a == 0 else 0] = one(i, c)
+            else:
+                row_share(a, i, one(i, c))
 
     def received(a, own):
-        total = own[...]
-        for j in range(1, mp_count):
-            m_copy(a, j).wait()
-            total = total + mp_recv[a, j - 1].astype(F32)
+        to_core(a, 0).wait_recv()
+        total = own[0] + mp_recv[a, 0].astype(F32)
+        for i in range(1, ys_count):
+            to_row(a, i).wait_recv()
+            total = total + mp_recv[a, ys_count + i - 1].astype(F32)
         return total
+
+    def shares_sent(a):
+        for i in range(ys_count):
+            to_core(a, i).wait_send()
+        for i in range(1, ys_count):
+            to_row(a, i).wait_send()
 
     pending = {}
     turn = [0]
@@ -495,9 +523,24 @@
             pending[slot] = copy
             turn[0] += 1
 
-    for h in range(halves):
-        rs_compute(2, h)
-        rs_start(2, h)
+    transposed(hg, ht)
+    for k in range(1, Z):
+        forward_c(1, k, True)
+    for k in range(1, Z):
+        ready(1, k, True)
+    transposed(dg, dt)
+    own_sent(0)
+    rest_sent(0)
+    rs_compute(2, 0)
+    rs_start(2, 0)
+    hidden_half(3, steps // 2, steps)
+    load_d = pltpu.make_async_copy(wd_hbm, wa, w_sem.at[0])
+    load_d.start()
+    at_once(inner & late, (pass_on, 2))
+    at_once(outer & late, (take, 2), (take, 3))
+    at_once(outer & alone, (take, 3))
+    rs_compute(2, 1)
+    rs_start(2, 1)
     load_d.wait()
 
     def gradient_part(k, first, last):
@@ -515,8 +558,6 @@
     forward_c(1, 1, False)
     gradient_part(0, 0, steps)
     forward_c(1, 2, False)
-    own_sent(1)
-    over_hidden(0, ((hidden, wa),), own_b, False)
     ready(1, 1, False)
     gradient_part(1, 0, steps)
     forward_c(1, 3, False)
@@ -527,25 +568,27 @@
     rs_compute(0, 0)
     rs_start(0, 0)
     gradient_part(Z - 1, steps // 2, steps)
+    rs_compute(1, 0)
+    rs_start(1, 0)
+    own_sent(1)
+    rest_sent(1)
+    over_hidden(0, ((hidden, wa),), own_b)
     load_g = pltpu.make_async_copy(wg_hbm, wa, w_sem.at[0])
     load_g.start()
-    rs_compute(1, 0)
-    rs_start(1, 0)
     rs_compute(0, 1)
     rs_start(0, 1)
     rs_compute(1, 1)
-    rest_sent(1)
     load_g.wait()
-    over_hidden(1, ((ggi, wa), (gl, wb)), own_g, True)
-    for j in range(1, mp_count):
-        m_copy(0, j).start()
+    over_hidden(1, ((ggi, wa), (gl, wb)), own_g)
+    for i in range(1, ys_count):
+        row_share(0, i, own_b[i])
     for w in range(3):
         own_rows(w)
     for copy in pending.values():
         copy.wait()
-    own_g[...] = received(1, own_g)
+    own_g[0] = received(1, own_g)
     normed = x_ref[...].astype(F32) * per_token(sblk[...])
-    part_x[x] = group_sums(own_g[...] * normed)
+    part_x[x] = group_sums(own_g[0] * normed)
     exchange_start(part_x, x, px_s, px_r, xs, x_peer)
     rs_start(1, 1)
     part_z[z] = exchange_sum(part_x, x, px_s, px_r, xs, x_peer)
@@ -556,9 +599,11 @@
     normed = x_ref[...].astype(F32) * scale
     mean_term = per_token(per_block(gain * total / GHOST))
     gt_ref[...] = (
-        dy_ref[...].astype(F32) + scale * (gain * own_g[...] - normed * mean_term)
+        dy_ref[...].astype(F32) + scale * (gain * own_g[0] - normed * mean_term)
     ).astype(BF16)
     bo_ref[...] = (x_ref[...].astype(F32) + received(0, own_b)).astype(BF16)
+    shares_sent(0)
+    shares_sent(1)
     for w in range(3):
         for j in range(1, xs):
             for h in range(halves):
@@ -626,11 +671,11 @@
             pltpu.VMEM((Z,) + table, F32),
             pltpu.VMEM((xs,) + table, F32),
             pltpu.VMEM((Z,) + table, F32),
-            pltpu.VMEM((rows_t, feat), F32),
-            pltpu.VMEM((rows_t, feat), F32),
+            pltpu.VMEM((ys_count, rows_t, feat), F32),
+            pltpu.VMEM((1, rows_t, feat), F32),
             dma((2,)),
-            dma((2, 5)),
-            dma((2, Z)),
+            dma((2, 6)),
+            dma((2, Z + 1)),
             dma((2, Z, ys_count)),
             dma((2, Z, ys_count)),
             dma((2, Z, ys_count)),

time: 158 us -> 155 us (0.981)
  Pallas kernels: 157 us -> 154 us
    pallas_call x1, Pallas kernels: 150 us -> 147 us  [body(): pl.pallas_call(functools.partial(kernel, tok_count, mp_count), out_shape=...]
where the time goes in v2:
time: 155 us
  Pallas kernels  154 us (99%)
    pallas_call x1, Pallas kernels, body(): pl.pallas_call(functools.partial(kernel, tok_count, mp_count), out_shape=...  147 us
    pallas_call x1, Pallas kernels, body(): pl.pallas_call(finish, grid=(width // span,), out_shape=small + (grad,) *...  7.07 us

profile of v2, /device:TPU:0, one launch (start us, length us, event | category | flops | bytes accessed | tf_op | source)
XLA Modules:
  0.0 154.6 jit_solution(9130924944013753547)
XLA Ops:
  0.6 146.9 %sublayer.1 = (bf16[384,512]{1,0:T(8,128)(2,1)}, bf16[384,512]{1,0:T(8,128)(2,1)}, f32[1,512]{1,0:T(1,128)}, f32[1,512]{1,0:T(1,128)}, f32[3,256,2048]{2,1,0:T(8,128)}, /*index=5*/bf16[3,1,256,2048]{3,2,1,0:T(8,128)(2,1)}) custom-call(bf16[384,512]{1,0:T(8,128)(2,1)} %x_ref.1, f32[4,1,512]{2,1,0:T(1,128)} %bitcast.5, f32[1,512]{1,0:T(1,128)} %bitcast.6, ...), custom_call_target="tpu_custom_call" | custom-call | tf_op jit(solution)/shard_map/sublayer/pallas_call | solution.py:648
  147.6 7.1 %finish.1 = (bf16[384,512]{1,0:T(8,128)(2,1)}, bf16[384,512]{1,0:T(8,128)(2,1)}, f32[1,512]{1,0:T(1,128)}, f32[1,512]{1,0:T(1,128)}, f32[256,2048]{1,0:T(8,128)}...) custom-call(f32[3,256,2048]{2,1,0:T(8,128)} %get-tuple-element.20.own, bf16[3,1,256,2048]{3,2,1,0:T(8,128)(2,1)} %get-tuple-element.21.recv, ...), custom_call_target="tpu_custom_call" | custom-call | tf_op jit(solution)/shard_map/finish/pallas_call | solution.py:715
